TPU v7x, 32 devices: a whole 2x2x4 slice. The times are simulated.
32 devices in a mesh: outer: 4 (over y, x), rep: 4 (over z), shard: 2 (over core).
Axes of the slice: x: 2, y: 2, z: 4, core: 2. Of those that a mesh axis runs over, the one named last changes fastest.
Arguments:
- deltas: bfloat16 [4, 4, 1024, 5120], P('outer', 'rep', 'shard'), may hold values from -1400 to 1400, as said below
- owners: int32 [2, 4, 1], P('shard'), may hold values from 0 to 3; in each aligned block of 4 rows (0 to 3, 4 to 7, ..., all dimensions but the last counted through in order) at most 2 rows name the same one
- master: float32 [4, 2, 2, 128, 5120], P('outer', 'shard', None, 'rep'), may hold values from -6 to 6
- momentum: float32 [4, 2, 2, 128, 5120], P('outer', 'shard', None, 'rep'), may hold values from -3 to 3
Outputs:
- new_params: bfloat16 [1024, 5120], P('shard')
- new_momentum: float32 [4, 2, 2, 128, 5120], P('outer', 'shard', None, 'rep')
- new_master: float32 [4, 2, 2, 128, 5120], P('outer', 'shard', None, 'rep')
Inputs may be any that keep to these rules, and one draw needn't show every extreme that they name: `owners`: within each shard, no pod owns more than 2 blocks, and in some shards one pod owns exactly 2. `deltas`: finite values.
All inputs are finite; a program needn't handle non-finite values.
Results may differ from a plain program's by a relative error of at most 0.0075.
Values may be sent and summed in bfloat16 or wider, within the bound.
A program may use at most 128 MiB of HBM per device.

v0:
```python
import math

import jax
import jax.numpy as jnp
from jax import lax
from jax.sharding import PartitionSpec as P


def local(deltas, owners, master, momentum):
    blocks_here = owners.shape[1]
    slot_count = master.shape[2]
    sub_rows = master.shape[3]
    row_width = deltas.shape[3]
    block_rows = deltas.shape[2] // blocks_here
    pod_count = lax.axis_size("outer")
    rep_count = lax.axis_size("rep")
    owned_blocks = owners[0, :, 0]
    pod_ids = jnp.arange(pod_count, dtype=jnp.int32)
    onehot = (owned_blocks[:, None] == pod_ids[None, :]).astype(jnp.int32)
    rank_all = jnp.cumsum(onehot, axis=0) - onehot
    rank_own = jnp.sum(rank_all * onehot, axis=1)
    slot_ids = jnp.arange(slot_count, dtype=jnp.int32)
    selector = (
        (owned_blocks[None, None, :] == pod_ids[:, None, None])
        & (rank_own[None, None, :] == slot_ids[None, :, None])
    ).astype(jnp.bfloat16)
    local_rows = deltas[0, 0].reshape(blocks_here, block_rows, row_width)
    block_sums = lax.psum_scatter(
        local_rows.astype(jnp.float32).astype(jnp.bfloat16), "rep", scatter_dimension=1, tiled=True
    ).astype(jnp.float32)
    block_sums = block_sums.astype(jnp.bfloat16)
    pod_part = jnp.einsum(
        "ojb,brw->ojrw", selector, block_sums, preferred_element_type=jnp.float32
    ).astype(jnp.bfloat16)
    arrived = lax.all_to_all(pod_part, "outer", split_axis=0, concat_axis=0, tiled=True)
    mean_share = jnp.sum(arrived.astype(jnp.float32), axis=0) / (pod_count * rep_count)
    local_sq = jnp.sum(mean_share * mean_share)
    total_sq = lax.psum(local_sq, ("outer", "rep", "shard"))
    total_entries = lax.axis_size("shard") * blocks_here * block_rows * row_width
    clip_limit = 0.5 * math.sqrt(total_entries)
    factor = jnp.minimum(1.0, clip_limit / jnp.sqrt(total_sq + 1e-06))
    step_part = factor * mean_share[None, None]
    new_momentum = 0.9 * momentum + step_part
    new_master = master - 0.7 * (step_part + 0.9 * new_momentum)
    params_here = new_master.astype(jnp.bfloat16)
    gathered = lax.all_gather(params_here, ("outer", "rep"), axis=0, tiled=True).reshape(
        pod_count, rep_count, slot_count, sub_rows, row_width
    )
    unpacked = jnp.einsum("ojb,oqjrw->bqrw", selector, gathered, preferred_element_type=jnp.float32)
    new_params = unpacked.astype(jnp.bfloat16).reshape(blocks_here * block_rows, row_width)
    return (new_params, new_momentum, new_master)


def solution(mesh):
    return jax.shard_map(
        local,
        mesh=mesh,
        in_specs=(
            P("outer", "rep", "shard", None),
            P("shard", None, None),
            P("outer", "shard", None, "rep", None),
            P("outer", "shard", None, "rep", None),
        ),
        out_specs=(
            P("shard", None),
            P("outer", "shard", None, "rep", None),
            P("outer", "shard", None, "rep", None),
        ),
        check_vma=False,
    )
```

profile of v0, /device:TPU:0, one launch (start us, length us, event | category | flops | bytes accessed | tf_op | source)
XLA Modules:
  0.0 455.7 jit_solution(926701552547225716)
XLA Ops:
  7.2 0.0 all-reduce.3.cloned.1.call-start
  7.2 8.9 %copy.26 = bf16[4,128,5120]{2,0,1:T(4,128)(2,1)} copy(bf16[4,128,5120]{2,1,0:T(8,128)(2,1)} %bitcast.30) | data formatting | bytes 10485760 | tf_op jit(solution)/shard_map/reshape;squeeze | solution.py:27
  16.1 0.0 all-reduce.3.cloned.1.call-update
  16.1 0.0 all-gather.2.cloned.1.call-start
  16.2 0.6 copy-done.2
  16.8 0.6 dynamic-slice
  18.0 0.0 copy-done.1
  18.0 0.1 fusion.6
  18.1 0.2 select_reduce_fusion
  18.3 0.1 iota_compare_fusion.1
  18.4 189.5 %all-reduce.3.cloned.1.call-done = bf16[4,128,5120]{2,0,1:T(4,128)(2,1)} async-done(((bf16[4,128,5120]{2,0,1:T(4,128)(2,1)}), bf16[4,128,5120]{2,0,1:T(4,128)(2,1)}) %all-reduce.3.cloned.1.call-update) | async-done | bytes 5242896
  207.9 3.0 convolution_convert_fusion
  210.9 0.8 copy.28
  211.7 34.3 %all_to_all.5 = bf16[4,2,32,5120]{3,2,1,0:T(8,128)(2,1)S(1)} all-to-all(bf16[4,2,32,5120]{3,2,1,0:T(8,128)(2,1)S(1)} %copy.28), channel_id=1, replica_groups=mesh['outer'=4,'rep'=4,'shard'=2] {'outer'}, dimensions={0} | all-to-all | bytes 5242880 | tf_op jit(solution)/shard_map/all_to_all | solution.py:35
  246.0 0.4 convert_reduce_fusion
  246.4 0.0 copy-start
  246.4 0.9 multiply_reduce_fusion
  247.4 38.6 %psum.7 = f32[]{:T(128)} all-reduce(f32[]{:T(128)} %multiply_reduce_fusion), channel_id=1, replica_groups=mesh['outer'=4,'rep'=4,'shard'=2] {'outer','rep','shard'}, use_global_device_ids=true, to_apply=%region_5.6 | all-reduce | flops 1 | bytes 8 | tf_op jit(solution)/shard_map/psum | solution.py:38
  286.6 0.0 copy-done
  286.7 3.4 fusion.12
  290.0 0.0 all-gather.2.cloned.1.call-update
  290.1 131.9 %all-gather.2.cloned.1.call-done = bf16[16,1,2,32,5120]{4,3,2,1,0:T(8,128)(2,1)} async-done(((bf16[1,1,2,32,5120]{4,3,2,1,0:T(8,128)(2,1)}), bf16[16,1,2,32,5120]{4,3,2,1,0:T(8,128)(2,1)}) %all-gather.2.cloned.1.call-update) | async-done | bytes 10485776 | tf_op jit(solution)/shard_map/all_gather | solution.py:46
  422.0 23.0 %bitcast_convert_fusion = bf16[4,4,32,5120]{3,0,2,1:T(4,128)(2,1)S(1)} fusion(bf16[4,4,2,32,5120]{4,3,2,1,0:T(8,128)(2,1)} %bitcast.35, pred[2,4]{1,0:T(4,128)(4,1)S(1)} %iota_compare_fusion.2, pred[4,4]{0,1:T(4,128)(4,1)S(1)} %iota_compare_fusion.1), kind=kOutput, calls=%fused_computation | convolution fusion | flops 44564512 | bytes 15728664 | tf_op jit(solution)/shard_map/ojb,oqjrw->bqrw/dot_general | solution.py:49
  444.9 3.9 copy.30
  (4 shorter events, 0.0 us)
Async XLA Ops:
  7.2 200.8 %all-reduce.3.cloned.1.call-start = ((), (), s32[]{:S(2)}) async-start(), calls=%async_computation.2 | async-start | bytes 10485760
  16.1 0.7 copy-start.2
  16.1 1.9 copy-start.1
  16.1 405.8 %all-gather.2.cloned.1.call-start = ((), (), s32[]{:S(2)}) async-start(), calls=%async_computation.1 | async-start | bytes 11141120 | tf_op jit(solution)/shard_map/all_gather | solution.py:46
  246.4 40.2 %copy-start = (f32[1,1,2,32,5120]{4,3,2,1,0:T(8,128)S(1)}, f32[1,1,2,32,5120]{4,3,2,1,0:T(8,128)}, u32[]{:S(2)}) copy-start(f32[1,1,2,32,5120]{4,3,2,1,0:T(8,128)} %param.6) | copy-start | bytes 3932164
Sparse Core Ops, SparseCore 0:
  16.2 191.6 all-reduce.2
  290.2 131.7 all-gather.1
where the time goes:
time: 456 us
  waiting for transfers between devices  321 us (70%)
  blocking collectives  72.8 us (16%)
  matrix products  26 us (6%)
  between operations  15.4 us (3%)
  local copies, waits for them, and re-layouts  14.7 us (3%)
  other arithmetic  5.11 us (1%)
    unnamed x3, waiting for transfers between devices  190 us
    all_gather x1, waiting for transfers between devices, local(): lax.all_gather(params_here, ('outer', 'rep'), axis=0, tiled=True)  132 us
    psum x1, blocking collectives, local(): total_sq = lax.psum(local_sq, ('outer', 'rep', 'shard'))  38.6 us
    all_to_all x1, blocking collectives, local(): lax.all_to_all(pod_part, 'outer', split_axis=0, concat_axis=0, tiled=True)  34.3 us
    dot_general x1, matrix products, local(): jnp.einsum('ojb,oqjrw->bqrw', selector, gathered, preferred_element_type=...  23 us
  transfers between devices with their start and end apart: 2, of which 2 were waited for; matrix products, arithmetic and copies ran while one was open for 0% of the time, Pallas kernels for 0%

commit v1 on v0

--- a/solution.py
+++ b/solution.py
@@ -1,9 +1,313 @@
+import functools
 import math
 
 import jax
 import jax.numpy as jnp
 from jax import lax
+from jax.experimental import pallas as pl
+from jax.experimental.pallas import tpu as pltpu
 from jax.sharding import PartitionSpec as P
+
+CHUNKS = 4
+TILE = 16
+SIDE = 2
+
+
+def ranks(owners, pod_count):
+    owned_blocks = owners[0, :, 0]
+    pod_ids = jnp.arange(pod_count, dtype=jnp.int32)
+    onehot = (owned_blocks[:, None] == pod_ids[None, :]).astype(jnp.int32)
+    rank_all = jnp.cumsum(onehot, axis=0) - onehot
+    return owned_blocks, jnp.sum(rank_all * onehot, axis=1)
+
+
+def kernel(
+    chunks, rep_count, shard_count, clip_limit,
+    sel, deltas, master, momentum,
+    out, new_momentum, new_master,
+    first, kept, passed, second, summed, third, mean, contrib, fourth, squares, others,
+    send_sem, recv_sem,
+):
+    blocks, slots, sub_rows, width = contrib.shape[0], master.shape[0], master.shape[1], master.shape[2]
+    block_rows = deltas.shape[2]
+    pod_count = SIDE * SIDE
+    half = width // 2
+    cols = half // chunks
+    o, q, s = lax.axis_index("outer"), lax.axis_index("rep"), lax.axis_index("shard")
+    y, x = o // SIDE, o % SIDE
+    x_pod, y_pod = y * SIDE + 1 - x, (1 - y) * SIDE + x
+
+    def pod(d):
+        return ((y + d // SIDE) % SIDE) * SIDE + (x + d % SIDE) % SIDE
+
+    barrier = pltpu.get_barrier_semaphore()
+    peers = [{"outer": pod(d)} for d in range(1, pod_count)]
+    peers += [{"rep": (q + d) % rep_count} for d in range(1, rep_count)]
+    peers += [{"shard": (s + d) % shard_count} for d in range(1, shard_count)]
+    for peer in peers:
+        pl.semaphore_signal(barrier, inc=1, device_id=peer, device_id_type=pl.DeviceIdType.MESH)
+    pl.semaphore_wait(barrier, len(peers))
+
+    started = []
+
+    def send(src, dst, **to):
+        number = len(started)
+        copy = pltpu.make_async_remote_copy(
+            src_ref=src, dst_ref=dst, send_sem=send_sem.at[number], recv_sem=recv_sem.at[number],
+            device_id=to, device_id_type=pl.DeviceIdType.MESH,
+        )
+        copy.start()
+        started.append(copy)
+        return copy
+
+    def tiles(rows, body):
+        def step(i, carry):
+            body(pl.ds(pl.multiple_of(i * TILE, TILE), TILE))
+            return carry
+
+        lax.fori_loop(0, rows // TILE, step, 0)
+
+    def left(c):
+        return pl.ds(c * cols, cols)
+
+    def right(c):
+        return pl.ds(half + c * cols, cols)
+
+    def pair(c):
+        return (left(c), right(c))
+
+    flight = {}
+
+    def send_first(c):
+        l, r = pair(c)
+        flight["first", c] = [
+            send(deltas.at[:, 1 - x, :, l], first.at[:, :, l], outer=x_pod),
+            send(deltas.at[1 - y, :, :, r], first.at[:, :, r], outer=y_pod),
+        ]
+
+    def send_second(c):
+        for copy in flight["first", c]:
+            copy.wait_recv()
+        l, r = pair(c)
+
+        def body(rows):
+            for at, go, stay in ((l, 1 - y, y), (r, 1 - x, x)):
+                own = (lambda k: deltas[k, x, rows, at]) if at is l else (lambda k: deltas[y, k, rows, at])
+                passed[rows, at] = (
+                    own(go).astype(jnp.float32) + first[go, rows, at].astype(jnp.float32)
+                ).astype(jnp.bfloat16)
+                kept[rows, at] = own(stay).astype(jnp.float32) + first[stay, rows, at].astype(jnp.float32)
+
+        tiles(block_rows, body)
+        flight["second", c] = [
+            send(passed.at[:, l], second.at[:, l], outer=y_pod),
+            send(passed.at[:, r], second.at[:, r], outer=x_pod),
+        ]
+
+    def send_third(c):
+        for copy in flight["second", c]:
+            copy.wait_recv()
+
+        def body(rows):
+            for at in pair(c):
+                total = kept[rows, at] + second[rows, at].astype(jnp.float32)
+                kept[rows, at] = total
+                summed[rows, at] = total.astype(jnp.bfloat16)
+
+        tiles(block_rows, body)
+        flight["third", c] = []
+        for at in pair(c):
+            for d in range(1, rep_count):
+                there = (q + d) % rep_count
+                rows = pl.ds(pl.multiple_of(there * sub_rows, sub_rows), sub_rows)
+                flight["third", c].append(send(summed.at[rows, at], third.at[d - 1, :, at], rep=there))
+
+    def take_mean(c):
+        for copy in flight["third", c]:
+            copy.wait_recv()
+
+        def body(rows):
+            mine = pl.ds(pl.multiple_of(q * sub_rows + rows.start, TILE), TILE)
+            for at in pair(c):
+                total = kept[mine, at]
+                for d in range(rep_count - 1):
+                    total = total + third[d, rows, at].astype(jnp.float32)
+                value = total * (1.0 / (pod_count * rep_count))
+                mean[o, rows, at] = value.astype(jnp.bfloat16)
+                square = value * value
+                part = squares[0]
+                for i in range(cols // 128):
+                    for k in range(TILE // 8):
+                        part = part + square[k * 8:(k + 1) * 8, i * 128:(i + 1) * 128]
+                squares[0] = part
+
+        tiles(sub_rows, body)
+
+    def send_mean(c):
+        flight["mean", c] = [
+            send(mean.at[o, :, at], mean.at[o, :, at], outer=pod(d))
+            for at in pair(c) for d in range(1, pod_count)
+        ]
+
+    squares[0] = jnp.zeros(squares.shape[1:], jnp.float32)
+    send_first(0)
+    send_first(1)
+    for t in range(chunks + 2):
+        if t < chunks:
+            send_second(t)
+        if t + 2 < chunks:
+            send_first(t + 2)
+        if 0 <= t - 1 < chunks:
+            send_third(t - 1)
+        if 0 <= t - 2 < chunks:
+            take_mean(t - 2)
+            if t - 2 < chunks - 1:
+                send_mean(t - 2)
+
+    number = 0
+    for level, (axis, count) in enumerate((("shard", shard_count), ("rep", rep_count), ("outer", pod_count))):
+        copies = []
+        for d in range(1, count):
+            there = {"shard": (s + d) % shard_count, "rep": (q + d) % rep_count, "outer": pod(d)}[axis]
+            copies.append(send(squares.at[level], others.at[number + d - 1], **{axis: there}))
+        if level == 0:
+            send_mean(chunks - 1)
+        total = squares[level]
+        for d, copy in enumerate(copies):
+            copy.wait_recv()
+            total = total + others[number + d]
+        number += count - 1
+        squares[level + 1] = total
+    total = jnp.sum(squares[3], keepdims=True)
+    factor = jnp.minimum(1.0, clip_limit / jnp.sqrt(total + 1e-06))
+
+    def update(c):
+        for copy in flight["mean", c]:
+            copy.wait_recv()
+
+        def body(rows):
+            for at in pair(c):
+                steps = [factor * mean[b, rows, at].astype(jnp.float32) for b in range(blocks)]
+                masters = []
+                for j in range(slots):
+                    step = sum(sel[b, j] * steps[b] for b in range(blocks))
+                    moved = 0.9 * momentum[j, rows, at] + step
+                    new_momentum[j, rows, at] = moved
+                    value = master[j, rows, at] - 0.7 * (step + 0.9 * moved)
+                    new_master[j, rows, at] = value
+                    masters.append(value)
+                for b in range(blocks):
+                    value = sum(sel[b, j] * masters[j] for j in range(slots))
+                    contrib[b, rows, at] = value.astype(jnp.bfloat16)
+
+        tiles(sub_rows, body)
+        flight["fourth", c] = []
+        for at in pair(c):
+            for d in range(1, pod_count):
+                flight["fourth", c].append(
+                    send(contrib.at[pod(d), :, at], fourth.at[d - 1, :, at], outer=pod(d))
+                )
+
+    def send_rows(c):
+        for copy in flight["fourth", c]:
+            copy.wait_recv()
+
+        def body(rows):
+            mine = pl.ds(pl.multiple_of(q * sub_rows + rows.start, TILE), TILE)
+            for at in pair(c):
+                value = contrib[o, rows, at].astype(jnp.float32)
+                for d in range(pod_count - 1):
+                    value = value + fourth[d, rows, at].astype(jnp.float32)
+                out[y, x, mine, at] = value.astype(jnp.bfloat16)
+
+        tiles(sub_rows, body)
+        rows = pl.ds(pl.multiple_of(q * sub_rows, sub_rows), sub_rows)
+        flight["rows", c] = [
+            send(out.at[y, x, rows, at], out.at[y, x, rows, at], rep=(q + d) % rep_count)
+            for at in pair(c) for d in range(1, rep_count)
+        ]
+
+    def send_block(c):
+        for copy in flight["rows", c]:
+            copy.wait_recv()
+        l, r = pair(c)
+        flight["block", c] = [
+            send(out.at[y, x, :, l], out.at[y, x, :, l], outer=x_pod),
+            send(out.at[y, x, :, r], out.at[y, x, :, r], outer=y_pod),
+        ]
+
+    def send_blocks(c):
+        for copy in flight["block", c]:
+            copy.wait_recv()
+        l, r = pair(c)
+        flight["blocks", c] = [
+            send(out.at[y, :, :, l], out.at[y, :, :, l], outer=y_pod),
+            send(out.at[:, x, :, r], out.at[:, x, :, r], outer=x_pod),
+        ]
+
+    for t in range(chunks + 3):
+        for lag, stage in enumerate((update, send_rows, send_block, send_blocks)):
+            if 0 <= t - lag < chunks:
+                stage(t - lag)
+    for c in range(chunks):
+        for copy in flight["blocks", c]:
+            copy.wait_recv()
+    for copy in started:
+        copy.wait_send()
+
+
+def fused(deltas, owners, master, momentum):
+    blocks = owners.shape[1]
+    slots, sub_rows, width = master.shape[2:]
+    block_rows = deltas.shape[2] // blocks
+    pod_count, rep_count = lax.axis_size("outer"), lax.axis_size("rep")
+    owned_blocks, rank_own = ranks(owners, pod_count)
+    mine = owned_blocks == lax.axis_index("outer")
+    sel = (mine[:, None] & (rank_own[:, None] == jnp.arange(slots)[None, :])).astype(jnp.float32)
+    clip_limit = 0.5 * math.sqrt(lax.axis_size("shard") * blocks * block_rows * width)
+    copies = CHUNKS * (4 + 2 * (rep_count - 1) + 4 * (pod_count - 1) + 2 * (rep_count - 1) + 4)
+    exchanged = lax.axis_size("shard") + rep_count + pod_count - 3
+    copies += exchanged
+    vmem = pl.BlockSpec(memory_space=pltpu.VMEM)
+    bf16, f32 = jnp.bfloat16, jnp.float32
+    out, new_momentum, new_master = pl.pallas_call(
+        functools.partial(kernel, CHUNKS, rep_count, lax.axis_size("shard"), clip_limit),
+        out_shape=(
+            jax.ShapeDtypeStruct((SIDE, SIDE, block_rows, width), bf16),
+            jax.ShapeDtypeStruct(master.shape[2:], f32),
+            jax.ShapeDtypeStruct(master.shape[2:], f32),
+        ),
+        in_specs=[pl.BlockSpec(memory_space=pltpu.SMEM), vmem, vmem, vmem],
+        out_specs=(vmem, vmem, vmem),
+        scratch_shapes=[
+            pltpu.VMEM((SIDE, block_rows, width), bf16),
+            pltpu.VMEM((block_rows, width), f32),
+            pltpu.VMEM((block_rows, width), bf16),
+            pltpu.VMEM((block_rows, width), bf16),
+            pltpu.VMEM((block_rows, width), bf16),
+            pltpu.VMEM((rep_count - 1, sub_rows, width), bf16),
+            pltpu.VMEM((blocks, sub_rows, width), bf16),
+            pltpu.VMEM((blocks, sub_rows, width), bf16),
+            pltpu.VMEM((pod_count - 1, sub_rows, width), bf16),
+            pltpu.VMEM((4, 8, 128), f32),
+            pltpu.VMEM((exchanged, 8, 128), f32),
+            pltpu.SemaphoreType.DMA((copies,)),
+            pltpu.SemaphoreType.DMA((copies,)),
+        ],
+        compiler_params=pltpu.CompilerParams(
+            collective_id=0, has_side_effects=True, vmem_limit_bytes=60 * 1024 * 1024
+        ),
+    )(
+        sel,
+        deltas.reshape(SIDE, SIDE, block_rows, width),
+        master.reshape(master.shape[2:]),
+        momentum.reshape(momentum.shape[2:]),
+    )
+    return (
+        out.reshape(blocks * block_rows, width),
+        new_momentum.reshape(momentum.shape),
+        new_master.reshape(master.shape),
+    )
 
 
 def local(deltas, owners, master, momentum):
@@ -52,8 +356,17 @@
 
 
 def solution(mesh):
+    fits = mesh.shape["outer"] == SIDE * SIDE
+
+    def body(deltas, owners, master, momentum):
+        blocks = owners.shape[1]
+        width, sub_rows = master.shape[4], master.shape[3]
+        whole = width % (2 * CHUNKS * 128) == 0 and sub_rows % TILE == 0
+        plan = fused if fits and whole and blocks == SIDE * SIDE else local
+        return plan(deltas, owners, master, momentum)
+
     return jax.shard_map(
-        local,
+        body,
         mesh=mesh,
         in_specs=(
             P("outer", "rep", "shard", None),

time: 456 us -> 151 us (0.33)
  waiting for transfers between devices: 321 us -> 0 us
  Pallas kernels: 0 us -> 139 us
  blocking collectives: 72.8 us -> 0 us
  matrix products: 26 us -> 0 us
  between operations: 15.4 us -> 0.65 us
  local copies, waits for them, and re-layouts: 14.7 us -> 8.13 us
    unnamed x3 -> x0, waiting for transfers between devices: 190 us -> none
    pallas_call x0 -> x1, Pallas kernels: none -> 139 us  [fused(): pl.pallas_call(functools.partial(kernel, CHUNKS, rep_count, lax.axis_size...]
    all_gather x1 -> x0, waiting for transfers between devices: 132 us -> none  [local(): lax.all_gather(params_here, ('outer', 'rep'), axis=0, tiled=True)]
    psum x1 -> x0, blocking collectives: 38.6 us -> none  [local(): total_sq = lax.psum(local_sq, ('outer', 'rep', 'shard'))]
    all_to_all x1 -> x0, blocking collectives: 34.3 us -> none  [local(): lax.all_to_all(pod_part, 'outer', split_axis=0, concat_axis=0, tiled=True)]
    dot_general x2 -> x0, matrix products: 26 us -> none  [the longest x1 23 us: local(): jnp.einsum('ojb,oqjrw->bqrw', selector, gathered, preferred_element_type=...]
    another operation x1 -> x0, local copies, waits for them, and re-layouts: 8.89 us -> none  [local(): local_rows = deltas[0, 0].reshape(blocks_here, block_rows, row_width)]
    unnamed x7, local copies, waits for them, and re-layouts: 1.17 us -> 8.13 us
  transfers between devices with their start and end apart: 2 -> 0, of which waited for: 2 -> 0; matrix products, arithmetic and copies ran while one was open for 0% -> 0% of each run, Pallas kernels for 0% -> 0%
where the time goes in v1:
time: 151 us; the launch traced here: 150 us
  Pallas kernels  139 us (92%)
  local copies, waits for them, and re-layouts  8.13 us (5%)
  other arithmetic  2.92 us (2%)
    pallas_call x1, Pallas kernels, fused(): pl.pallas_call(functools.partial(kernel, CHUNKS, rep_count, lax.axis_size...  139 us
    unnamed x7, local copies, waits for them, and re-layouts  8.13 us

profile of v1, /device:TPU:0, one launch (start us, length us, event | category | flops | bytes accessed | tf_op | source)
XLA Modules:
  0.0 150.3 jit_solution(3613515182044308666)
XLA Ops:
  0.6 0.7 broadcast_compare_fusion
  1.3 0.7 fusion
  2.1 0.8 select_reduce_fusion
  2.9 0.7 fusion.2.sel
  3.6 138.6 %shard_map.67 = (bf16[2,2,128,5120]{3,2,1,0:T(8,128)(2,1)}, f32[2,32,5120]{2,1,0:T(8,128)}, f32[2,32,5120]{2,1,0:T(8,128)}) custom-call(f32[4,2]{1,0:T(4,128)} %fusion.2.sel, bf16[2,2,128,5120]{3,2,1,0:T(8,128)(2,1)} %bitcast.8, f32[2,32,5120]{2,1,0:T(8,128)} %bitcast.12, f32[2,32,5120]{2,1,0:T(8,128)} %bitcast.13), custom_call_target="tpu_custom_call" | custom-call | tf_op jit(solution)/shard_map/pallas_call | solution.py:273
  142.1 0.0 copy-start.1
  142.1 5.3 %copy.10 = bf16[512,5120]{1,0:T(8,128)(2,1)} copy(bf16[512,5120]{1,0:T(8,128)(2,1)} %bitcast.9) | data formatting | bytes 10485760
  147.4 0.0 copy-done.1
  147.4 0.0 copy-start
  147.4 1.1 copy.11
  148.5 0.7 copy-done
  149.2 1.1 copy.12
  (1 shorter events, 0.0 us)
Async XLA Ops:
  142.1 5.3 %copy-start.1 = (f32[2,32,5120]{2,1,0:T(8,128)S(1)}, f32[2,32,5120]{2,1,0:T(8,128)}, u32[]{:S(2)}) copy-start(f32[2,32,5120]{2,1,0:T(8,128)} %get-tuple-element.7) | copy-start | bytes 3932164
  147.4 1.8 %copy-start = (f32[2,32,5120]{2,1,0:T(8,128)S(1)}, f32[2,32,5120]{2,1,0:T(8,128)}, u32[]{:S(2)}) copy-start(f32[2,32,5120]{2,1,0:T(8,128)} %get-tuple-element.8) | copy-start | bytes 3932164

commit v2 on v1

--- a/solution.py
+++ b/solution.py
@@ -8,7 +8,7 @@
 from jax.experimental.pallas import tpu as pltpu
 from jax.sharding import PartitionSpec as P
 
-CHUNKS = 4
+CHUNKS = 5
 TILE = 16
 SIDE = 2
 

time: 151 us -> 152 us (level)
  no operation moved by 1% of the time
where the time goes in v2:
time: 152 us; the launch traced here: 151 us
  Pallas kernels  140 us (92%)
  local copies, waits for them, and re-layouts  8.13 us (5%)
  other arithmetic  2.92 us (2%)
    pallas_call x1, Pallas kernels, fused(): pl.pallas_call(functools.partial(kernel, CHUNKS, rep_count, lax.axis_size...  140 us
    unnamed x7, local copies, waits for them, and re-layouts  8.13 us

profile of v2, /device:TPU:0, one launch (start us, length us, event | category | flops | bytes accessed | tf_op | source)
XLA Modules:
  0.0 151.4 jit_solution(16191310839412961618)
XLA Ops:
  0.6 0.7 broadcast_compare_fusion
  1.3 0.7 fusion
  2.1 0.8 select_reduce_fusion
  2.9 0.7 fusion.2.sel
  3.6 139.7 %shard_map.67 = (bf16[2,2,128,5120]{3,2,1,0:T(8,128)(2,1)}, f32[2,32,5120]{2,1,0:T(8,128)}, f32[2,32,5120]{2,1,0:T(8,128)}) custom-call(f32[4,2]{1,0:T(4,128)} %fusion.2.sel, bf16[2,2,128,5120]{3,2,1,0:T(8,128)(2,1)} %bitcast.8, f32[2,32,5120]{2,1,0:T(8,128)} %bitcast.12, f32[2,32,5120]{2,1,0:T(8,128)} %bitcast.13), custom_call_target="tpu_custom_call" | custom-call | tf_op jit(solution)/shard_map/pallas_call | solution.py:273
  143.3 0.0 copy-start.1
  143.3 5.3 %copy.10 = bf16[512,5120]{1,0:T(8,128)(2,1)} copy(bf16[512,5120]{1,0:T(8,128)(2,1)} %bitcast.9) | data formatting | bytes 10485760
  148.5 0.0 copy-done.1
  148.5 0.0 copy-start
  148.6 1.1 copy.11
  149.6 0.7 copy-done
  150.3 1.1 copy.12
  (1 shorter events, 0.0 us)
Async XLA Ops:
  143.3 5.3 %copy-start.1 = (f32[2,32,5120]{2,1,0:T(8,128)S(1)}, f32[2,32,5120]{2,1,0:T(8,128)}, u32[]{:S(2)}) copy-start(f32[2,32,5120]{2,1,0:T(8,128)} %get-tuple-element.7) | copy-start | bytes 3932164
  148.5 1.8 %copy-start = (f32[2,32,5120]{2,1,0:T(8,128)S(1)}, f32[2,32,5120]{2,1,0:T(8,128)}, u32[]{:S(2)}) copy-start(f32[2,32,5120]{2,1,0:T(8,128)} %get-tuple-element.8) | copy-start | bytes 3932164
